TPU v7x, 32 devices: a whole 2x2x4 slice. The times are simulated.
32 devices in a mesh: rep: 2 (over x), tp: 4 (over y, core), sub: 4 (over z).
Axes of the slice: x: 2, y: 2, z: 4, core: 2. Of those that a mesh axis runs over, the one named last changes fastest.
Arguments:
- acts: bfloat16 [2048, 16384], P(('rep', 'tp'), 'sub'), parts along dimension 0, may hold values from -6 to 6
- q_src: bfloat16 [32768, 16384], P(('rep', 'sub'), 'tp'), parts along dimension 0, may hold values from -0.046875 to 0.046875
- kv_src: bfloat16 [32768, 2048], P(('rep', 'sub'), 'tp'), parts along dimension 0, may hold values from -0.046875 to 0.046875
- q_src_heads: int32 [128], replicated, may hold values from 0 to 127, as said below
- q_tgt_heads: int32 [128], replicated, may hold values from 0 to 127, as said below
- kv_tgt_heads: int32 [16], replicated, may hold values from 0 to 7, as said below
Outputs:
- q_new: bfloat16 [32768, 16384], P(('rep', 'sub'), 'tp'), parts along dimension 0
- kv_new: bfloat16 [32768, 4096], P(('rep', 'sub'), 'tp'), parts along dimension 0
- qkv: bfloat16 [2048, 20480], P(('rep', 'sub'), 'tp'), parts along dimension 0
There are 2 independent parts, one for each index of `rep`. A program takes and returns all parts, laid end to end along the dimension named above; an argument that names none is the same for every part. Nothing has to cross between parts.
Inputs may be any that keep to these rules, and one draw needn't show every extreme that they name: q_src_heads and q_tgt_heads are permutations. Source block t is entries t * 32 to (t + 1) * 32 - 1 of q_src_heads, target block j the same entries of q_tgt_heads. With s = 1, source block t shares exactly 8 heads with target block (t + min(1, s - 1)) mod 4 and with each target block (t + k * s) mod 4 for k from 1 to 3, and none with any other. `q_tgt_heads`: see q_src_heads. `kv_tgt_heads`: every key-value head appears exactly twice.
All inputs are finite; a program needn't handle non-finite values.
Results may differ from a plain program's by a relative error of at most 0.001.
Values may be sent and summed in bfloat16 or wider, within the bound.
A program may use at most 256 MiB of HBM per device.

v0:
```python
import jax
import jax.numpy as jnp
from jax import lax
from jax.sharding import PartitionSpec as P

HD = 128


def per_device(acts, q_src, kv_src, q_src_heads, q_tgt_heads, kv_tgt_heads):
    tp_count = lax.axis_size("tp")
    my_index = lax.axis_index("tp")
    row_count = q_src.shape[0]
    q_local = q_src.shape[1] // HD
    capacity = max(2, q_local // tp_count)
    head_count = q_src_heads.shape[0]
    head_ids = jnp.arange(head_count, dtype=jnp.int32)
    matches = (q_src_heads[None, :] == q_tgt_heads[:, None]).astype(jnp.int32)
    target_pos = jnp.sum(matches * head_ids[:, None], axis=0)
    slot_of = jnp.sum(matches * head_ids[None, :], axis=1)
    target_dev = target_pos // q_local
    source_dev = head_ids // q_local
    earlier = (
        (source_dev[:, None] == source_dev[None, :])
        & (target_dev[:, None] == target_dev[None, :])
        & (head_ids[None, :] < head_ids[:, None])
    )
    slot_rank = jnp.sum(earlier.astype(jnp.int32), axis=1)
    own_target = lax.dynamic_slice_in_dim(target_dev, my_index * q_local, q_local)
    own_rank = lax.dynamic_slice_in_dim(slot_rank, my_index * q_local, q_local)
    buffer_ids = jnp.arange(tp_count * capacity, dtype=jnp.int32)
    slot_hit = ((own_target * capacity + own_rank)[None, :] == buffer_ids[:, None]).astype(
        jnp.int32
    )
    pick_slot = jnp.sum(slot_hit * jnp.arange(q_local, dtype=jnp.int32)[None, :], axis=1)
    filled = jnp.sum(slot_hit, axis=1) > 0
    my_slots = lax.dynamic_slice_in_dim(slot_of, my_index * q_local, q_local)
    receive_ids = my_slots // q_local * capacity + slot_rank[my_slots]

    def pack_heads(weights):
        leading = weights.shape[0]
        three = weights.reshape(leading, q_local, HD)
        packed = jnp.take(three, pick_slot, axis=1) * filled[None, :, None].astype(weights.dtype)
        return packed.reshape(leading, tp_count, capacity * HD)

    def unpack_heads(arrived):
        leading = arrived.shape[0]
        three = arrived.reshape(leading, tp_count * capacity, HD)
        return jnp.take(three, receive_ids, axis=1).reshape(leading, q_local * HD)

    q_arrived = lax.all_to_all(pack_heads(q_src), "tp", split_axis=1, concat_axis=1, tiled=True)
    q_new = unpack_heads(q_arrived)
    kv_slots = kv_tgt_heads.shape[0] // tp_count
    kv_whole = lax.all_gather(kv_src, "tp", axis=1, tiled=True)
    own_kv = lax.dynamic_slice_in_dim(kv_tgt_heads, my_index * kv_slots, kv_slots)
    kv_three = kv_whole.reshape(row_count, kv_whole.shape[1] // (2 * HD), 2 * HD)
    kv_new = jnp.take(kv_three, own_kv, axis=1).reshape(row_count, kv_slots * 2 * HD)
    gathered = lax.all_gather(acts, "tp", axis=0, tiled=True)

    def projector(weights):
        return jnp.dot(gathered, weights, preferred_element_type=jnp.float32)

    q_out = lax.psum_scatter(projector(q_src), "sub", scatter_dimension=0, tiled=True).astype(
        jnp.bfloat16
    )
    q_moved = lax.all_to_all(pack_heads(q_out), "tp", split_axis=1, concat_axis=1, tiled=True)
    kv_out = lax.psum_scatter(projector(kv_new), "sub", scatter_dimension=0, tiled=True).astype(
        jnp.bfloat16
    )
    qkv = jnp.concatenate([unpack_heads(q_moved), kv_out], axis=1)
    return (q_new, kv_new, qkv)


def solution(mesh):
    in_specs = (
        P(("rep", "tp"), "sub"),
        P(("rep", "sub"), "tp"),
        P(("rep", "sub"), "tp"),
        P(),
        P(),
        P(),
    )
    out_specs = (P(("rep", "sub"), "tp"), P(("rep", "sub"), "tp"), P(("rep", "sub"), "tp"))
    return jax.shard_map(
        per_device, mesh=mesh, in_specs=in_specs, out_specs=out_specs, check_vma=False
    )
```

profile of v0, /device:TPU:0, one launch (start us, length us, event | category | flops | bytes accessed | tf_op | source)
XLA Modules:
  0.0 703.1 jit_solution(10137896972993409188)
XLA Ops:
  7.2 0.0 all-gather.5.cloned.1.call-start
  7.2 0.7 all-gather.5.cloned.1.call-update
  7.9 0.0 all-gather.3.cloned.1.call-start
  7.9 0.7 all-gather.3.cloned.1.call-update
  8.6 0.0 reduce-scatter.3.cloned.1.call-start
  8.7 61.9 %all-gather.5.cloned.1.call-done = bf16[1024,4096]{1,0:T(8,128)(2,1)} async-done(((bf16[256,4096]{1,0:T(8,128)(2,1)}), bf16[1024,4096]{1,0:T(8,128)(2,1)}) %all-gather.5.cloned.1.call-update) | async-done | bytes 8388624 | tf_op jit(solution)/shard_map/all_gather | solution.py:57
  70.6 43.0 %fusion.4 = f32[1024,4096]{1,0:T(8,128)} fusion(bf16[1024,4096]{1,0:T(8,128)(2,1)} %all-gather.5.cloned.1.call-done, bf16[4096,4096]{1,0:T(8,128)(2,1)} %param.11), kind=kOutput, calls=%fused_computation.53 | convolution fusion | flops 34359738368 | bytes 58720256 | tf_op jit(solution)/shard_map/dot_general | solution.py:60
  113.5 0.0 reduce-scatter.3.cloned.1.call-update
  113.6 0.0 copy-start
  113.6 0.0 copy-start.1
  113.6 44.2 %copy.27 = bf16[4096,4096]{0,1:T(8,128)(2,1)} copy(bf16[4096,4096]{1,0:T(8,128)(2,1)} %param.11) | data formatting | bytes 67108864 | tf_op args[1]
  157.7 0.0 copy-done
  157.7 0.0 copy-done.1
  157.8 0.2 fusion.1
  157.9 0.2 convert_reduce_fusion
  158.1 0.1 dynamic-slice_add_fusion
  158.2 0.1 convert_reduce_fusion.1
  158.4 22.9 %gather_fusion.3 = bf16[32,4096,128]{1,2,0:T(8,128)(2,1)} fusion(bf16[4096,32,128]{0,2,1:T(8,128)(2,1)} %bitcast.31, s32[1024]{0:T(1024)S(1)} %pad_clamp_fusion.2), kind=kCustom, calls=%fused_computation.clone | custom fusion | bytes 67108992 | tf_op jit(solution)/shard_map/jit(_take)/gather | solution.py:42
  181.3 22.3 %bitcast_multiply_fusion = bf16[4096,32,128]{0,2,1:T(8,128)(2,1)} fusion(bf16[32,4096,128]{1,2,0:T(8,128)(2,1)} %gather_fusion.3, pred[32]{0:T(512)(128)(4,1)S(1)} %compare_and_fusion.1, bf16[32]{0:T(256)(128)(2,1)S(1)} %compare_convert_fusion), kind=kLoop, calls=%fused_computation.7 | loop fusion | flops 33554432 | bytes 67108960 | tf_op jit(solution)/shard_map/mul | solution.py:42
  203.5 0.0 copy-start.2
  203.5 9.9 %all-to-all-start = ((bf16[4096,4,1024]{0,2,1:T(8,128)(2,1)}), bf16[4096,4,1024]{0,2,1:T(8,128)(2,1)}, u32[]{:S(2)}, u32[]{:S(2)}) async-start(bf16[4096,4,1024]{0,2,1:T(8,128)(2,1)} %bitcast.33), calls=%async_computation | async-start | bytes 67108864 | tf_op jit(solution)/shard_map/all_to_all | solution.py:50
  213.5 0.2 reduce-scatter.5.cloned.1.call-start
  213.7 0.0 copy-done.2
  213.7 0.1 compare_and_fusion.2
  213.8 0.1 broadcast_in_dim.53
  213.9 0.0 all-gather.3.cloned.1.call-done
  213.9 12.0 %fusion.3 = (bf16[2048,2048]{1,0:T(8,128)(2,1)}, bf16[2048,2048]{1,0:T(8,128)(2,1)}) fusion(bf16[4096,2048]{1,0:T(8,128)(2,1)} %all-gather.3.cloned.1.call-done), kind=kLoop, calls=%fused_computation.52 | loop fusion | bytes 33554432 | tf_op jit(solution)/shard_map/jit(_take)/gather | solution.py:56
  226.0 12.3 %copy.29 = bf16[2048,2048]{0,1:T(8,128)(2,1)} copy(bf16[2048,2048]{1,0:T(8,128)(2,1)} %get-tuple-element.23) | data formatting | bytes 16777216 | tf_op jit(solution)/shard_map/jit(_take)/gather | solution.py:56
  238.2 12.5 %copy.28 = bf16[2048,2048]{0,1:T(8,128)(2,1)} copy(bf16[2048,2048]{1,0:T(8,128)(2,1)} %get-tuple-element.22) | data formatting | bytes 16777216 | tf_op jit(solution)/shard_map/jit(_take)/gather | solution.py:56
  250.7 6.5 gather_fusion.2
  257.1 6.4 gather_fusion.1
  263.5 8.0 %pad_maximum_fusion = bf16[4096,4,256]{0,2,1:T(8,128)(2,1)} fusion(bf16[2048,4,256]{0,2,1:T(8,128)(2,1)} %bitcast.37, bf16[2048,4,256]{0,2,1:T(8,128)(2,1)} %bitcast.38), kind=kLoop, calls=%fused_computation.9 | loop fusion | flops 16777216 | bytes 16777216
  271.5 12.0 %copy.30 = bf16[4096,1024]{1,0:T(8,128)(2,1)} copy(bf16[4096,1024]{0,1:T(8,128)(2,1)} %bitcast.34) | data formatting | bytes 16777216 | tf_op jit(solution)/shard_map/jit(_take)/gather | solution.py:56
  283.4 7.5 %broadcast_select_fusion.1 = bf16[4096,1024]{1,0:T(8,128)(2,1)} fusion(bf16[4096,1024]{1,0:T(8,128)(2,1)} %copy.30, pred[1024]{0:T(1024)(128)(4,1)S(1)} %broadcast_in_dim.54), kind=kLoop, calls=%fused_computation.10 | loop fusion | flops 4194304 | bytes 16778240 | tf_op jit(solution)/shard_map/jit(_take)/select_n | solution.py:56
  290.9 15.2 %convolution_bitcast_fusion = f32[1024,1024]{0,1:T(8,128)} fusion(bf16[4096,1024]{1,0:T(8,128)(2,1)} %broadcast_select_fusion.1, bf16[1024,4096]{1,0:T(8,128)(2,1)} %all-gather.5.cloned.1.call-done), kind=kOutput, calls=%fused_computation.12 | convolution fusion | flops 8589934592 | bytes 20971520 | tf_op jit(solution)/shard_map/dot_general | solution.py:60
  306.2 0.0 reduce-scatter.5.cloned.1.call-update
  306.2 0.1 compare_select_fusion.5
  306.3 0.7 gather_fusion
  307.0 0.1 compare_and_fusion
  307.1 269.2 %all-to-all-done = bf16[4096,4,1024]{0,2,1:T(8,128)(2,1)} async-done(((bf16[4096,4,1024]{0,2,1:T(8,128)(2,1)}), bf16[4096,4,1024]{0,2,1:T(8,128)(2,1)}, u32[]{:S(2)}, u32[]{:S(2)}) %all-to-all-start) | async-done | bytes 33554464 | tf_op jit(solution)/shard_map/all_to_all | solution.py:50
  576.3 23.0 %gather_fusion.4 = bf16[32,4096,128]{1,2,0:T(8,128)(2,1)} fusion(bf16[4096,32,128]{0,2,1:T(8,128)(2,1)} %bitcast.3, s32[1024]{0:T(1024)S(1)} %pad_clamp_fusion.1), kind=kCustom, calls=%fused_computation.2.clone | custom fusion | bytes 67108992 | tf_op jit(solution)/shard_map/jit(_take)/gather | solution.py:48
  599.3 0.0 reduce-scatter.3.cloned.1.call-done
  599.3 2.7 copy_bitcast_fusion
  602.0 2.1 gather_fusion.5
  604.1 1.9 bitcast_multiply_fusion.1
  606.0 2.9 copy.32
  608.9 3.8 all-to-all-start.1
  612.8 22.8 %broadcast_select_fusion = bf16[32,4096,128]{1,2,0:T(8,128)(2,1)} fusion(bf16[32,4096,128]{1,2,0:T(8,128)(2,1)} %gather_fusion.4, pred[32]{0:T(512)(128)(4,1)S(1)} %get-tuple-element.20), kind=kLoop, calls=%fused_computation.8 | loop fusion | flops 16777216 | bytes 67108896 | tf_op jit(solution)/shard_map/jit(_take)/select_n | solution.py:48
  635.6 44.1 %copy.35 = bf16[4096,4096]{1,0:T(8,128)(2,1)} copy(bf16[4096,4096]{0,1:T(8,128)(2,1)} %bitcast.32) | data formatting | bytes 67108864
  679.7 0.0 reduce-scatter.5.cloned.1.call-done
  679.7 1.3 convert_element_type.26
  681.0 0.0 all-to-all-done.1
  681.0 2.9 copy.33
  683.8 2.5 gather_fusion.6
  686.4 1.6 select_bitcast_fusion
  688.0 4.1 copy.34
  692.0 1.8 pad_maximum_fusion.1
  693.8 2.8 copy.36
  (9 shorter events, 0.1 us)
Async XLA Ops:
  7.2 63.4 %all-gather.5.cloned.1.call-start = ((), (), s32[]{:S(2)}) async-start(), calls=%async_computation.5 | async-start | bytes 10485760 | tf_op jit(solution)/shard_map/all_gather | solution.py:57
  7.9 206.0 %all-gather.3.cloned.1.call-start = ((), (), s32[]{:S(2)}) async-start(), calls=%async_computation.4 | async-start | bytes 20971520 | tf_op jit(solution)/shard_map/all_gather | solution.py:53
  8.6 590.7 %reduce-scatter.3.cloned.1.call-start = ((), (), s32[]{:S(2)}) async-start(), calls=%async_computation.6 | async-start | bytes 20971520 | tf_op jit(solution)/shard_map/reduce_scatter | solution.py:62
  113.6 44.2 %copy-start = (s32[128]{0:T(128)S(1)}, s32[128]{0:T(128)}, u32[]{:S(2)}) copy-start(s32[128]{0:T(128)} %param.13) | copy-start | bytes 1540
  113.6 44.2 %copy-start.1 = (s32[128]{0:T(128)S(1)}, s32[128]{0:T(128)}, u32[]{:S(2)}) copy-start(s32[128]{0:T(128)} %param.14) | copy-start | bytes 1540
  203.5 10.2 %copy-start.2 = (s32[16]{0:T(128)S(1)}, s32[16]{0:T(128)}, u32[]{:S(2)}) copy-start(s32[16]{0:T(128)} %param.15) | copy-start | bytes 196
  203.5 372.7 %all-to-all-start = ((bf16[4096,4,1024]{0,2,1:T(8,128)(2,1)}), bf16[4096,4,1024]{0,2,1:T(8,128)(2,1)}, u32[]{:S(2)}, u32[]{:S(2)}) async-start(bf16[4096,4,1024]{0,2,1:T(8,128)(2,1)} %bitcast.33), calls=%async_computation | async-start | bytes 67108864 | tf_op jit(solution)/shard_map/all_to_all | solution.py:50
  213.5 466.2 %reduce-scatter.5.cloned.1.call-start = ((), (), s32[]{:S(2)}) async-start(), calls=%async_computation.7 | async-start | bytes 5242880 | tf_op jit(solution)/shard_map/reduce_scatter | solution.py:66
  608.9 72.0 %all-to-all-start.1 = ((bf16[256,4,1024]{0,2,1:T(8,128)(2,1)}), bf16[256,4,1024]{0,2,1:T(8,128)(2,1)S(1)}, u32[]{:S(2)}, u32[]{:S(2)}) async-start(bf16[256,4,1024]{0,2,1:T(8,128)(2,1)} %bitcast.40), calls=%async_computation.2 | async-start | bytes 4194304 | tf_op jit(solution)/shard_map/all_to_all | solution.py:65
Sparse Core Ops, SparseCore 0:
  9.5 60.9 all-gather.4
  72.1 105.8 all-gather.2
  180.4 280.4 reduce-scatter.2
  463.0 77.3 reduce-scatter.4
where the time goes:
time: 707 us; the launch traced here: 703 us
  waiting for transfers between devices  332 us (47%)
  local copies, waits for them, and re-layouts  214 us (30%)
  other arithmetic  70.6 us (10%)
  matrix products  58.2 us (8%)
  starting transfers between devices  14.1 us (2%)
  between operations  13.9 us (2%)
    all_to_all x1, waiting for transfers between devices, per_device(): lax.all_to_all(pack_heads(q_src), 'tp', split_axis=1, concat_axis=1, tile...  269 us
    unnamed x9, local copies, waits for them, and re-layouts  91 us
    all_gather x1, waiting for transfers between devices, per_device(): gathered = lax.all_gather(acts, 'tp', axis=0, tiled=True)  61.9 us
    gather x6, local copies, waits for them, and re-layouts, per_device(): jnp.take(kv_three, own_kv, axis=1).reshape(row_count, kv_slots * 2 * HD)  61.5 us
    dot_general x2, matrix products, projector(): return jnp.dot(gathered, weights, preferred_element_type=jnp.float32)  58.2 us
    gather x2, local copies, waits for them, and re-layouts, unpack_heads(): return jnp.take(three, receive_ids, axis=1).reshape(leading, q_local * HD)  25.6 us
    gather x2, local copies, waits for them, and re-layouts, pack_heads(): jnp.take(three, pick_slot, axis=1)  25 us
    select_n x2, other arithmetic, unpack_heads(): return jnp.take(three, receive_ids, axis=1).reshape(leading, q_local * HD)  24.4 us
  transfers between devices with their start and end apart: 6, of which 2 were waited for; matrix products, arithmetic and copies ran while one was open for 47% of the time, Pallas kernels for 0%

commit v1 on v0

--- a/solution.py
+++ b/solution.py
@@ -47,7 +47,12 @@
         three = arrived.reshape(leading, tp_count * capacity, HD)
         return jnp.take(three, receive_ids, axis=1).reshape(leading, q_local * HD)
 
-    q_arrived = lax.all_to_all(pack_heads(q_src), "tp", split_axis=1, concat_axis=1, tiled=True)
+    q_arrived = jnp.concatenate(
+        lax.all_to_all(
+            jnp.stack(jnp.split(pack_heads(q_src), lax.axis_size("tp"), 1), 0), "tp", 0, 0
+        ),
+        axis=1,
+    )
     q_new = unpack_heads(q_arrived)
     kv_slots = kv_tgt_heads.shape[0] // tp_count
     kv_whole = lax.all_gather(kv_src, "tp", axis=1, tiled=True)

time: 707 us -> 844 us (1.19)
  local copies, waits for them, and re-layouts: 214 us -> 326 us
  other arithmetic: 70.6 us -> 95.5 us
    unnamed x9 -> x25, local copies, waits for them, and re-layouts: 91 us -> 140 us
    reshape x0 -> x1, local copies, waits for them, and re-layouts: none -> 40.5 us  [per_device(): jnp.concatenate(lax.all_to_all(jnp.stack(jnp.split(pack_heads(q_src), lax...]
    split x0 -> x1, local copies, waits for them, and re-layouts: none -> 23.2 us  [per_device(): jnp.split(pack_heads(q_src), lax.axis_size('tp'), 1)]
    another operation x0 -> x1, other arithmetic: none -> 22.8 us  [per_device(): jnp.stack(jnp.split(pack_heads(q_src), lax.axis_size('tp'), 1), 0)]
  transfers between devices with their start and end apart: 6 -> 6, of which waited for: 2 -> 2; matrix products, arithmetic and copies ran while one was open for 47% -> 55% of each run, Pallas kernels for 0% -> 0%
where the time goes in v1:
time: 844 us; the launch traced here: 838 us
  waiting for transfers between devices  330 us (39%)
  local copies, waits for them, and re-layouts  326 us (39%)
  other arithmetic  95.5 us (11%)
  matrix products  58.4 us (7%)
  between operations  14 us (2%)
  starting transfers between devices  13.9 us (2%)
    all_to_all x1, waiting for transfers between devices, per_device(): lax.all_to_all(jnp.stack(jnp.split(pack_heads(q_src), lax.axis_size('tp')...  269 us
    unnamed x25, local copies, waits for them, and re-layouts  140 us
    gather x6, local copies, waits for them, and re-layouts, per_device(): jnp.take(kv_three, own_kv, axis=1).reshape(row_count, kv_slots * 2 * HD)  61.3 us
    all_gather x1, waiting for transfers between devices, per_device(): gathered = lax.all_gather(acts, 'tp', axis=0, tiled=True)  59.7 us
    dot_general x2, matrix products, projector(): return jnp.dot(gathered, weights, preferred_element_type=jnp.float32)  58.4 us
    reshape x1, local copies, waits for them, and re-layouts, per_device(): jnp.concatenate(lax.all_to_all(jnp.stack(jnp.split(pack_heads(q_src), lax...  40.5 us
    gather x2, local copies, waits for them, and re-layouts, unpack_heads(): return jnp.take(three, receive_ids, axis=1).reshape(leading, q_local * HD)  25.4 us
    gather x2, local copies, waits for them, and re-layouts, pack_heads(): jnp.take(three, pick_slot, axis=1)  25.1 us
  transfers between devices with their start and end apart: 6, of which 2 were waited for; matrix products, arithmetic and copies ran while one was open for 55% of the time, Pallas kernels for 0%

profile of v1, /device:TPU:0, one launch (start us, length us, event | category | flops | bytes accessed | tf_op | source)
XLA Modules:
  0.0 837.9 jit_solution(7530825441867822553)
XLA Ops:
  7.2 0.0 all-gather.5.cloned.1.call-start
  7.2 0.7 all-gather.5.cloned.1.call-update
  7.9 0.0 all-gather.3.cloned.1.call-start
  7.9 0.7 all-gather.3.cloned.1.call-update
  8.6 0.0 reduce-scatter.3.cloned.1.call-start
  8.7 1.4 fusion.1
  10.1 0.2 convert_reduce_fusion
  10.3 0.5 copy-done
  10.7 0.1 dynamic-slice_add_fusion
  10.8 59.7 %all-gather.5.cloned.1.call-done = bf16[1024,4096]{1,0:T(8,128)(2,1)} async-done(((bf16[256,4096]{1,0:T(8,128)(2,1)}), bf16[1024,4096]{1,0:T(8,128)(2,1)}) %all-gather.5.cloned.1.call-update) | async-done | bytes 8388624 | tf_op jit(solution)/shard_map/all_gather | solution.py:62
  70.6 43.0 %fusion.5 = f32[1024,4096]{1,0:T(8,128)} fusion(bf16[1024,4096]{1,0:T(8,128)(2,1)} %all-gather.5.cloned.1.call-done, bf16[4096,4096]{1,0:T(8,128)(2,1)} %param.11), kind=kOutput, calls=%fused_computation.55 | convolution fusion | flops 34359738368 | bytes 58720256 | tf_op jit(solution)/shard_map/dot_general | solution.py:65
  113.5 0.0 reduce-scatter.3.cloned.1.call-update
  113.5 0.1 convert_reduce_fusion.1
  113.7 44.1 %copy.40 = bf16[4096,4096]{0,1:T(8,128)(2,1)} copy(bf16[4096,4096]{1,0:T(8,128)(2,1)} %param.11) | data formatting | bytes 67108864 | tf_op args[1]
  157.8 22.9 %gather_fusion.3 = bf16[32,4096,128]{1,2,0:T(8,128)(2,1)} fusion(bf16[4096,32,128]{0,2,1:T(8,128)(2,1)} %bitcast.36, s32[1024]{0:T(1024)S(1)} %pad_clamp_fusion.2), kind=kCustom, calls=%fused_computation.clone | custom fusion | bytes 67108992 | tf_op jit(solution)/shard_map/jit(_take)/gather | solution.py:42
  180.7 0.0 copy-done.2
  180.7 0.0 copy-start.4
  180.7 0.0 copy-start.6
  180.7 23.2 %bitcast_multiply_fusion = bf16[4096,32,128]{0,2,1:T(8,128)(2,1)} fusion(bf16[32,4096,128]{1,2,0:T(8,128)(2,1)} %gather_fusion.3, pred[32]{0:T(512)(128)(4,1)S(1)} %compare_and_fusion.1, bf16[32]{0:T(256)(128)(2,1)S(1)} %compare_convert_fusion), kind=kLoop, calls=%fused_computation.8 | loop fusion | flops 33554432 | bytes 67108960 | tf_op jit(solution)/shard_map/mul | solution.py:42
  203.9 0.0 copy-done.4
  204.0 23.2 %fusion.3 = (bf16[4096,1,1024]{0,2,1:T(8,128)(2,1)}, bf16[4096,1,1024]{0,2,1:T(8,128)(2,1)}, bf16[4096,1,1024]{0,2,1:T(8,128)(2,1)}, bf16[4096,1,1024]{0,2,1:T(8,128)(2,1)}) fusion(bf16[4096,4,1024]{0,2,1:T(8,128)(2,1)} %bitcast.39), kind=kLoop, calls=%fused_computation.53 | loop fusion | bytes 67108864 | tf_op jit(solution)/shard_map/split | solution.py:52
  227.2 12.0 %copy.58 = bf16[4096,1,1024]{2,0,1:T(8,128)(2,1)} copy(bf16[4096,1,1024]{0,2,1:T(8,128)(2,1)} %get-tuple-element.25) | data formatting | bytes 16777216
  239.2 12.0 %copy.57 = bf16[4096,1,1024]{2,0,1:T(8,128)(2,1)} copy(bf16[4096,1,1024]{0,2,1:T(8,128)(2,1)} %get-tuple-element.23) | data formatting | bytes 16777216
  251.2 12.1 %copy.56 = bf16[4096,1,1024]{2,0,1:T(8,128)(2,1)} copy(bf16[4096,1,1024]{0,2,1:T(8,128)(2,1)} %get-tuple-element.24) | data formatting | bytes 16777216
  263.3 11.9 %copy.55 = bf16[4096,1,1024]{2,0,1:T(8,128)(2,1)} copy(bf16[4096,1,1024]{0,2,1:T(8,128)(2,1)} %get-tuple-element.22) | data formatting | bytes 16777216
  275.3 22.8 %pad_maximum_fusion = bf16[4,4096,1,1024]{3,1,2,0:T(8,128)(2,1)} fusion(bf16[1,4096,1,1024]{3,1,2,0:T(8,128)(2,1)} %bitcast.41, bf16[1,4096,1,1024]{3,1,2,0:T(8,128)(2,1)} %bitcast.42, bf16[1,4096,1,1024]{3,1,2,0:T(8,128)(2,1)} %bitcast.43, bf16[1,4096,1,1024]{3,1,2,0:T(8,128)(2,1)} %bitcast.44), kind=kLoop, calls=%fused_computation.7 | loop fusion | flops 50331648 | bytes 67108864 | tf_op jit(solution)/shard_map/stack | solution.py:52
  298.1 0.0 copy-start.8
  298.1 9.8 %all-to-all-start = ((bf16[4,4096,1,1024]{3,1,2,0:T(8,128)(2,1)}), bf16[4,4096,1,1024]{3,1,2,0:T(8,128)(2,1)}, u32[]{:S(2)}, u32[]{:S(2)}) async-start(bf16[4,4096,1,1024]{3,1,2,0:T(8,128)(2,1)} %pad_maximum_fusion), calls=%async_computation | async-start | bytes 67108864 | tf_op jit(solution)/shard_map/all_to_all | solution.py:51
  307.9 0.2 reduce-scatter.5.cloned.1.call-start
  308.1 0.1 compare_and_fusion.2
  308.2 0.1 broadcast_in_dim.53
  308.3 0.0 all-gather.3.cloned.1.call-done
  308.3 12.1 %fusion.4 = (bf16[2048,2048]{1,0:T(8,128)(2,1)}, bf16[2048,2048]{1,0:T(8,128)(2,1)}) fusion(bf16[4096,2048]{1,0:T(8,128)(2,1)} %all-gather.3.cloned.1.call-done), kind=kLoop, calls=%fused_computation.54 | loop fusion | bytes 33554432 | tf_op jit(solution)/shard_map/jit(_take)/gather | solution.py:61
  320.4 12.4 %copy.47 = bf16[2048,2048]{0,1:T(8,128)(2,1)} copy(bf16[2048,2048]{1,0:T(8,128)(2,1)} %get-tuple-element.27) | data formatting | bytes 16777216 | tf_op jit(solution)/shard_map/jit(_take)/gather | solution.py:61
  332.8 12.4 %copy.46 = bf16[2048,2048]{0,1:T(8,128)(2,1)} copy(bf16[2048,2048]{1,0:T(8,128)(2,1)} %get-tuple-element.26) | data formatting | bytes 16777216 | tf_op jit(solution)/shard_map/jit(_take)/gather | solution.py:61
  345.2 6.2 gather_fusion.2
  351.4 6.2 gather_fusion.1
  357.6 8.0 pad_maximum_fusion.1
  365.6 12.1 %copy.48 = bf16[4096,1024]{1,0:T(8,128)(2,1)} copy(bf16[4096,1024]{0,1:T(8,128)(2,1)} %bitcast.40) | data formatting | bytes 16777216 | tf_op jit(solution)/shard_map/jit(_take)/gather | solution.py:61
  377.6 7.5 broadcast_select_fusion.1
  385.1 15.4 %convolution_bitcast_fusion = f32[1024,1024]{0,1:T(8,128)} fusion(bf16[4096,1024]{1,0:T(8,128)(2,1)} %broadcast_select_fusion.1, bf16[1024,4096]{1,0:T(8,128)(2,1)} %all-gather.5.cloned.1.call-done), kind=kOutput, calls=%fused_computation.13 | convolution fusion | flops 8589934592 | bytes 20971520 | tf_op jit(solution)/shard_map/dot_general | solution.py:65
  400.5 0.0 reduce-scatter.5.cloned.1.call-update
  400.6 0.1 compare_select_fusion.5
  400.7 0.7 gather_fusion
  401.4 0.1 compare_and_fusion
  401.5 269.2 %all-to-all-done = bf16[4,4096,1,1024]{3,1,2,0:T(8,128)(2,1)} async-done(((bf16[4,4096,1,1024]{3,1,2,0:T(8,128)(2,1)}), bf16[4,4096,1,1024]{3,1,2,0:T(8,128)(2,1)}, u32[]{:S(2)}, u32[]{:S(2)}) %all-to-all-start) | async-done | bytes 33554464 | tf_op jit(solution)/shard_map/all_to_all | solution.py:51
  670.7 40.5 %copy.45 = bf16[4096,4,1,1024]{0,3,1,2:T(8,128)(2,1)} copy(bf16[4096,4,1,1024]{3,0,2,1:T(8,128)(2,1)} %bitcast.7) | data formatting | bytes 67108864 | tf_op jit(solution)/shard_map/reshape | solution.py:50
  711.1 22.8 %gather_fusion.4 = bf16[32,4096,128]{1,2,0:T(8,128)(2,1)} fusion(bf16[4096,32,128]{0,2,1:T(8,128)(2,1)} %bitcast.37, s32[1024]{0:T(1024)S(1)} %pad_clamp_fusion.1), kind=kCustom, calls=%fused_computation.2.clone | custom fusion | bytes 67108992 | tf_op jit(solution)/shard_map/jit(_take)/gather | solution.py:48
  734.0 2.7 copy_bitcast_fusion
  736.7 2.3 gather_fusion.5
  739.0 0.0 copy-done.5
  739.0 1.9 bitcast_multiply_fusion.1
  740.9 2.9 copy.50
  743.7 3.8 all-to-all-start.1
  747.6 22.8 %broadcast_select_fusion = bf16[32,4096,128]{1,2,0:T(8,128)(2,1)} fusion(bf16[32,4096,128]{1,2,0:T(8,128)(2,1)} %gather_fusion.4, pred[32]{0:T(512)(128)(4,1)S(1)} %get-tuple-element.20), kind=kLoop, calls=%fused_computation.9 | loop fusion | flops 16777216 | bytes 67108896 | tf_op jit(solution)/shard_map/jit(_take)/select_n | solution.py:48
  770.4 44.1 %copy.53 = bf16[4096,4096]{1,0:T(8,128)(2,1)} copy(bf16[4096,4096]{0,1:T(8,128)(2,1)} %bitcast.38) | data formatting | bytes 67108864
  814.5 1.3 convert_element_type.26
  815.8 0.0 all-to-all-done.1
  815.8 2.9 copy.51
  818.7 2.5 gather_fusion.6
  821.2 1.6 select_bitcast_fusion
  822.8 4.1 copy.52
  826.8 1.8 pad_maximum_fusion.2
  828.6 2.8 copy.54
  (22 shorter events, 0.1 us)
Async XLA Ops:
  7.2 63.4 %all-gather.5.cloned.1.call-start = ((), (), s32[]{:S(2)}) async-start(), calls=%async_computation.5 | async-start | bytes 10485760 | tf_op jit(solution)/shard_map/all_gather | solution.py:62
  7.9 300.4 %all-gather.3.cloned.1.call-start = ((), (), s32[]{:S(2)}) async-start(), calls=%async_computation.4 | async-start | bytes 20971520 | tf_op jit(solution)/shard_map/all_gather | solution.py:58
  8.6 725.3 %reduce-scatter.3.cloned.1.call-start = ((), (), s32[]{:S(2)}) async-start(), calls=%async_computation.6 | async-start | bytes 20971520 | tf_op jit(solution)/shard_map/reduce_scatter | solution.py:67
  10.3 0.5 copy-start
  157.8 22.9 %copy-start.2 = (s32[1024]{0:T(1024)}, s32[1024]{0:T(1024)S(1)}, u32[]{:S(2)}) copy-start(s32[1024]{0:T(1024)S(1)} %pad_clamp_fusion.2) | copy-start | bytes 12292
  180.7 23.2 %copy-start.4 = (pred[32]{0:T(512)(128)(4,1)}, pred[32]{0:T(512)(128)(4,1)S(1)}, u32[]{:S(2)}) copy-start(pred[32]{0:T(512)(128)(4,1)S(1)} %compare_and_fusion.1) | copy-start | bytes 100
  180.7 23.2 %copy-start.6 = (bf16[32]{0:T(256)(128)(2,1)}, bf16[32]{0:T(256)(128)(2,1)S(1)}, u32[]{:S(2)}) copy-start(bf16[32]{0:T(256)(128)(2,1)S(1)} %compare_convert_fusion) | copy-start | bytes 196
  298.1 10.0 %copy-start.8 = (s32[16]{0:T(128)S(1)}, s32[16]{0:T(128)}, u32[]{:S(2)}) copy-start(s32[16]{0:T(128)} %param.15) | copy-start | bytes 196
  298.1 372.6 %all-to-all-start = ((bf16[4,4096,1,1024]{3,1,2,0:T(8,128)(2,1)}), bf16[4,4096,1,1024]{3,1,2,0:T(8,128)(2,1)}, u32[]{:S(2)}, u32[]{:S(2)}) async-start(bf16[4,4096,1,1024]{3,1,2,0:T(8,128)(2,1)} %pad_maximum_fusion), calls=%async_computation | async-start | bytes 67108864 | tf_op jit(solution)/shard_map/all_to_all | solution.py:51
  307.9 506.6 %reduce-scatter.5.cloned.1.call-start = ((), (), s32[]{:S(2)}) async-start(), calls=%async_computation.7 | async-start | bytes 5242880 | tf_op jit(solution)/shard_map/reduce_scatter | solution.py:71
  385.1 15.4 %copy-start.3 = (s32[128]{0:T(128)S(1)}, s32[128]{0:T(128)}, u32[]{:S(2)}) copy-start(s32[128]{0:T(128)} %get-tuple-element.14) | copy-start | bytes 1540
  385.1 15.5 %copy-start.1 = (s32[128]{0:T(128)S(1)}, s32[128]{0:T(128)}, u32[]{:S(2)}) copy-start(s32[128]{0:T(128)} %copy-done) | copy-start | bytes 1540
  734.0 5.0 copy-start.5
  734.0 5.0 copy-start.7
  743.7 72.0 %all-to-all-start.1 = ((bf16[256,4,1024]{0,2,1:T(8,128)(2,1)}), bf16[256,4,1024]{0,2,1:T(8,128)(2,1)S(1)}, u32[]{:S(2)}, u32[]{:S(2)}) async-start(bf16[256,4,1024]{0,2,1:T(8,128)(2,1)} %bitcast.50), calls=%async_computation.2 | async-start | bytes 4194304 | tf_op jit(solution)/shard_map/all_to_all | solution.py:70
Sparse Core Ops, SparseCore 0:
  9.5 60.9 all-gather.4
  72.1 105.8 all-gather.2
  180.4 280.4 reduce-scatter.2
  463.0 77.3 reduce-scatter.4
